TPU v7x, 32 devices: a whole 2x2x4 slice. The times are simulated.
32 devices in a mesh: dp: 2 (over x), tp: 16 (over y, z, core).
Axes of the slice: x: 2, y: 2, z: 4, core: 2. Of those that a mesh axis runs over, the one named last changes fastest.
Arguments:
- x: bfloat16 [128, 4608], P('dp'), parts along dimension 0
- k_cache: bfloat16 [128, 4096, 16, 128], P('dp', None, 'tp'), parts along dimension 0
- v_cache: bfloat16 [128, 4096, 16, 128], P('dp', None, 'tp'), parts along dimension 0
- gain_a: bfloat16 [4608], replicated
- wq: bfloat16 [4608, 4096], P(None, 'tp')
- wo: bfloat16 [4096, 4608], P('tp')
- gain_m: bfloat16 [4608], replicated
- w_gate: bfloat16 [4608, 36864], P(None, 'tp')
- w_up: bfloat16 [4608, 36864], P(None, 'tp')
- w_down: bfloat16 [36864, 4608], P('tp')
Outputs:
- output: bfloat16 [128, 4608], P('dp'), parts along dimension 0
There are 2 independent parts. A program takes and returns all parts, laid end to end along the dimension named above; an argument that names none is the same for every part.
All inputs are finite; a program needn't handle non-finite values.
Results may differ from a plain program's by a relative error of at most 0.017.
Values are sent between devices in bfloat16 or wider.
A program may use at most 2 GiB of HBM per device.

v0:
```python
import jax
import jax.numpy as jnp
from jax import lax
from jax.sharding import PartitionSpec as P

HEAD = 128
THETA = 10000


def normed(x, gain):
    wide = x.astype(jnp.float32)
    scale = lax.rsqrt(jnp.mean(wide * wide, -1, keepdims=True) + 1e-6)
    return (wide * scale * gain.astype(jnp.float32)).astype(jnp.bfloat16)


def turned(t, place, theta):
    half = t.shape[-1] // 2
    angle = place.astype(jnp.float32)[:, None] * theta ** (-jnp.arange(half, dtype=jnp.float32) / half)
    cos, sin = jnp.cos(angle)[:, None], jnp.sin(angle)[:, None]
    a, b = t[..., :half].astype(jnp.float32), t[..., half:].astype(jnp.float32)
    return jnp.concatenate([a * cos - b * sin, b * cos + a * sin], -1).astype(jnp.bfloat16)


def matmul(a, w):
    return jnp.dot(a, w, preferred_element_type=jnp.float32).astype(jnp.bfloat16)


def einsum(form, a, b):
    return jnp.einsum(form, a.astype(jnp.float32), b.astype(jnp.float32))


def seen_by(a, wq, k_cache, v_cache, head, theta):
    batch, cache, kv_heads = k_cache.shape[:3]
    place = jnp.full((batch,), cache - 1)
    q = turned(matmul(a, wq).reshape(batch, -1, head), place, theta).reshape(batch, kv_heads, -1, head)
    scores = einsum("bgsd,bugd->bgsu", q, k_cache) * head**-0.5
    weights = jax.nn.softmax(scores, -1).astype(jnp.bfloat16)
    return einsum("bgsu,bugd->bgsd", weights, v_cache).astype(jnp.bfloat16).reshape(batch, -1)


def hidden_of(b, w_gate, w_up):
    gate = jnp.dot(b, w_gate, preferred_element_type=jnp.float32)
    up = jnp.dot(b, w_up, preferred_element_type=jnp.float32)
    return (jax.nn.silu(gate) * up).astype(jnp.bfloat16)


def solution(mesh):
    def added(t, term):
        return (t.astype(jnp.float32) + lax.psum(term.astype(jnp.bfloat16), "tp").astype(jnp.float32)).astype(jnp.bfloat16)

    def step(x, k_cache, v_cache, gain_a, wq, wo, gain_m, w_gate, w_up, w_down):
        seen = seen_by(normed(x, gain_a), wq, k_cache, v_cache, HEAD, THETA)
        h = added(x, jnp.dot(seen, wo, preferred_element_type=jnp.float32))
        return added(h, jnp.dot(hidden_of(normed(h, gain_m), w_gate, w_up), w_down, preferred_element_type=jnp.float32))

    states, cache, columns, rows_of = P("dp", None), P("dp", None, "tp", None), P(None, "tp"), P("tp", None)
    return jax.shard_map(
        step,
        mesh=mesh,
        in_specs=(states, cache, cache, P(None), columns, rows_of, P(None), columns, columns, rows_of),
        out_specs=states,
        check_vma=False,
    )
```

profile of v0, /device:TPU:0, one launch (start us, length us, event | category | flops | bytes accessed | tf_op | source)
XLA Modules:
  0.0 284.7 jit_solution(419732631716667982)
XLA Ops:
  6.6 0.9 convert_element_type.66
  7.5 1.3 fusion.11
  8.7 2.4 convolution_convert_fusion.2
  11.2 0.1 fusion.39
  11.4 0.1 pad_maximum_fusion
  11.5 27.1 %fusion.40 = (f32[64,2]{1,0:T(8,128)S(1)}, f32[64,2,4096]{2,1,0:T(2,128)}) fusion(bf16[64,4096,1,128]{3,1,2,0:T(8,128)(2,1)} %param.11, bf16[64,2,128]{2,0,1:T(8,128)(2,1)S(1)} %pad_maximum_fusion), kind=kOutput, calls=%fused_computation.51 | convolution fusion | flops 135794688 | bytes 69239296 | tf_op jit(solution)/shard_map/sub | solution.py:37
  38.6 23.3 %fusion.19 = bf16[64,2,128]{2,1,0:T(2,128)(2,1)S(1)} fusion(bf16[64,4096,1,128]{3,1,2,0:T(8,128)(2,1)} %param.12, f32[64,2,4096]{2,1,0:T(2,128)} %get-tuple-element.12, f32[64,2]{1,0:T(8,128)S(1)} %get-tuple-element.11), kind=kOutput, calls=%fused_computation.27 | convolution fusion | flops 135282688 | bytes 69239296 | tf_op jit(solution)/shard_map/bgsu,bugd->bgsd/dot_general | solution.py:29
  61.9 0.0 copy-start.3
  61.9 0.0 copy-start.1
  61.9 1.4 convolution_convert_fusion.1
  63.3 0.0 all-reduce.3.cloned.1.call-update
  63.3 0.2 all-reduce.5.cloned.1.call-start
  63.6 0.6 convert_element_type.77
  64.2 93.9 %all-reduce.3.cloned.1.call-done = bf16[64,4608]{1,0:T(8,128)(2,1)} async-done(((bf16[64,4608]{1,0:T(8,128)(2,1)}), bf16[64,4608]{1,0:T(8,128)(2,1)}) %all-reduce.3.cloned.1.call-update) | async-done | bytes 589840 | tf_op jit(solution)/shard_map/psum | solution.py:49
  158.1 1.4 fusion.15
  159.5 0.0 slice-start
  159.5 0.0 slice-start.1
  159.5 9.3 %fusion.27 = f32[64,2304]{1,0:T(8,128)S(1)} fusion(bf16[4608,2304]{1,0:T(8,128)(2,1)} %param.17, bf16[64,4608]{1,0:T(8,128)(2,1)S(1)} %get-tuple-element.6, f32[4608]{0:T(1024)} %convert_element_type.77, f32[64]{0:T(128)S(1)} %add_rsqrt_fusion), kind=kOutput, calls=%fused_computation.32 | convolution fusion | flops 1360134144 | bytes 22432000 | tf_op jit(solution)/shard_map/dot_general | solution.py:42
  168.8 0.0 slice-start.3
  168.8 11.3 %fusion.10 = bf16[64,2304]{1,0:T(8,128)(2,1)S(1)} fusion(bf16[4608,2304]{1,0:T(8,128)(2,1)} %param.18, f32[64,2304]{1,0:T(8,128)S(1)} %fusion.27, bf16[64,4608]{1,0:T(8,128)(2,1)S(1)} %get-tuple-element.6, f32[4608]{0:T(1024)S(1)} %copy-done.2, f32[64]{0:T(128)S(1)} %add_rsqrt_fusion), kind=kOutput, calls=%fused_computation.11 | convolution fusion | flops 1361018880 | bytes 22726912 | tf_op jit(solution)/shard_map/dot_general | solution.py:43
  180.2 4.6 %convolution_convert_fusion = bf16[64,4608]{1,0:T(8,128)(2,1)} fusion(bf16[64,2304]{1,0:T(8,128)(2,1)S(1)} %fusion.10, bf16[2304,4608]{1,0:T(8,128)(2,1)S(1)} %bitcast.23), kind=kOutput, calls=%fused_computation.5 | convolution fusion | flops 1359249408 | bytes 22118400 | tf_op jit(solution)/shard_map/dot_general | solution.py:54
  184.8 0.0 all-reduce.5.cloned.1.call-update
  184.9 91.0 %all-reduce.5.cloned.1.call-done = bf16[64,4608]{1,0:T(8,128)(2,1)} async-done(((bf16[64,4608]{1,0:T(8,128)(2,1)}), bf16[64,4608]{1,0:T(8,128)(2,1)}) %all-reduce.5.cloned.1.call-update) | async-done | bytes 589840 | tf_op jit(solution)/shard_map/psum | solution.py:49
  275.8 2.0 fusion.18
  (22 shorter events, 0.1 us)
Async XLA Ops:
  6.5 55.4 %copy-start = (bf16[256,4608]{1,0:T(8,128)(2,1)S(1)}, bf16[256,4608]{1,0:T(8,128)(2,1)}, u32[]{:S(2)}) copy-start(bf16[256,4608]{1,0:T(8,128)(2,1)} %param.15) | copy-start | bytes 7077892
  6.5 151.5 %all-reduce.3.cloned.1.call-start = ((), (), s32[]{:S(2)}) async-start(), calls=%async_computation | async-start | bytes 1179648 | tf_op jit(solution)/shard_map/psum | solution.py:49
  61.9 1.6 copy-start.3
  61.9 96.1 %copy-start.1 = (bf16[64,4608]{1,0:T(8,128)(2,1)S(1)}, bf16[64,4608]{1,0:T(8,128)(2,1)}, u32[]{:S(2)}) copy-start(bf16[64,4608]{1,0:T(8,128)(2,1)} %param.10) | copy-start | bytes 1769476
  63.3 212.5 %all-reduce.5.cloned.1.call-start = ((), (), s32[]{:S(2)}) async-start(), calls=%async_computation.1 | async-start | bytes 1179648 | tf_op jit(solution)/shard_map/psum | solution.py:49
  159.5 9.3 %copy-start.2 = (f32[4608]{0:T(1024)S(1)}, f32[4608]{0:T(1024)}, u32[]{:S(2)}) copy-start(f32[4608]{0:T(1024)} %convert_element_type.77) | copy-start | bytes 55300
  159.5 20.7 %slice-start = ((s8[21233664]{0:T(1024)(128)(4,1)}), s8[4194304]{0:T(1024)(128)(4,1)S(1)}, s32[]{:S(2)}) async-start(s8[21233664]{0:T(1024)(128)(4,1)} %bitcast.22), calls=%async_computation.2 | async-start | bytes 8388608
  159.5 20.7 %slice-start.1 = ((s8[21233664]{0:T(1024)(128)(4,1)}), s8[4194304]{0:T(1024)(128)(4,1)S(1)}, s32[]{:S(2)}) async-start(s8[21233664]{0:T(1024)(128)(4,1)} %bitcast.22), calls=%async_computation.3 | async-start | bytes 8388608
  159.5 20.7 %slice-start.2 = ((s8[21233664]{0:T(1024)(128)(4,1)}), s8[4194304]{0:T(1024)(128)(4,1)S(1)}, s32[]{:S(2)}) async-start(s8[21233664]{0:T(1024)(128)(4,1)} %bitcast.22), calls=%async_computation.4 | async-start | bytes 8388608
  168.8 11.4 %slice-start.3 = ((s8[21233664]{0:T(1024)(128)(4,1)}), s8[4194304]{0:T(1024)(128)(4,1)S(1)}, s32[]{:S(2)}) async-start(s8[21233664]{0:T(1024)(128)(4,1)} %bitcast.22), calls=%async_computation.5 | async-start | bytes 8388608
  168.8 11.4 %slice-start.4 = ((s8[21233664]{0:T(1024)(128)(4,1)}), s8[4194304]{0:T(1024)(128)(4,1)S(1)}, s32[]{:S(2)}) async-start(s8[21233664]{0:T(1024)(128)(4,1)} %bitcast.22), calls=%async_computation.6 | async-start | bytes 8388608
  168.8 11.4 %slice-start.5 = ((s8[21233664]{0:T(1024)(128)(4,1)}), s8[262144]{0:T(1024)(128)(4,1)S(1)}, s32[]{:S(2)}) async-start(s8[21233664]{0:T(1024)(128)(4,1)} %bitcast.22), calls=%async_computation.7 | async-start | bytes 524288
Sparse Core Ops, SparseCore 0:
  63.4 94.5 all-reduce.2
  185.0 90.7 all-reduce.4
where the time goes:
time: 285 us
  waiting for transfers between devices  185 us (65%)
  matrix products  79.5 us (28%)
  between operations  13.6 us (5%)
  other arithmetic  6.3 us (2%)
    psum x2, waiting for transfers between devices, added(): lax.psum(term.astype(jnp.bfloat16), 'tp').astype(jnp.float32)  185 us
    sub x1, matrix products, seen_by(): weights = jax.nn.softmax(scores, -1).astype(jnp.bfloat16)  27.1 us
    dot_general x1, matrix products, einsum(): return jnp.einsum(form, a.astype(jnp.float32), b.astype(jnp.float32))  23.3 us
    dot_general x1, matrix products, hidden_of(): up = jnp.dot(b, w_up, preferred_element_type=jnp.float32)  11.3 us
    dot_general x1, matrix products, hidden_of(): gate = jnp.dot(b, w_gate, preferred_element_type=jnp.float32)  9.27 us
  transfers between devices with their start and end apart: 2, of which 2 were waited for; matrix products, arithmetic and copies ran while one was open for 0% of the time, Pallas kernels for 0%

commit v1 on v0

--- a/solution.py
+++ b/solution.py
@@ -1,10 +1,16 @@
+import functools
+
 import jax
 import jax.numpy as jnp
 from jax import lax
+from jax.experimental import pallas as pl
+from jax.experimental.pallas import tpu as pltpu
 from jax.sharding import PartitionSpec as P
 
 HEAD = 128
 THETA = 10000
+MESH = pl.DeviceIdType.MESH
+F32, BF16 = jnp.float32, jnp.bfloat16
 
 
 def normed(x, gain):
@@ -44,14 +50,87 @@
     return (jax.nn.silu(gate) * up).astype(jnp.bfloat16)
 
 
+def add_kernel(chips, t_ref, x_ref, o_ref, r0, s1, r1, a_send, a_recv, b_send, b_recv, c_send, c_recv, d_send, d_recv):
+    wide = t_ref.shape[2] // 2
+    me = lax.axis_index("tp")
+    core, chip = me % 2, me // 2
+    partner = me + 1 - 2 * core
+    own = pl.ds(pl.multiple_of(core * wide, 128), wide)
+    other = pl.ds(pl.multiple_of((1 - core) * wide, 128), wide)
+
+    def to(o):
+        return (chip + o) % chips
+
+    def frm(o):
+        return (chip + chips - o) % chips
+
+    def remote(src, dst, send, recv, device):
+        return pltpu.make_async_remote_copy(src_ref=src, dst_ref=dst, send_sem=send, recv_sem=recv, device_id={"tp": device}, device_id_type=MESH)
+
+    barrier = pltpu.get_barrier_semaphore()
+    pl.semaphore_signal(barrier, inc=1, device_id={"tp": partner}, device_id_type=MESH)
+    for o in range(1, chips):
+        pl.semaphore_signal(barrier, inc=1, device_id={"tp": to(o) * 2 + core}, device_id_type=MESH)
+    pl.semaphore_wait(barrier, chips)
+
+    halves = [remote(t_ref.at[to(o), :, other], r0.at[o], a_send.at[o], a_recv.at[o], partner) for o in range(chips)]
+    order = list(range(1, chips)) + [0]
+    for o in order:
+        halves[o].start()
+    terms = [None] + [remote(s1.at[o], r1.at[o], b_send.at[o], b_recv.at[o], to(o) * 2 + core) for o in range(1, chips)]
+    for o in range(1, chips):
+        halves[o].wait_recv()
+        s1[o] = (t_ref[to(o), :, own].astype(F32) + r0[o].astype(F32)).astype(BF16)
+        terms[o].start()
+    halves[0].wait_recv()
+    total = t_ref[chip, :, own].astype(F32) + r0[0].astype(F32)
+    for o in range(1, chips):
+        terms[o].wait_recv()
+        total = total + r1[o].astype(F32)
+    o_ref[chip, :, own] = (x_ref[chip, :, own].astype(F32) + total).astype(BF16)
+    done = o_ref.at[chip, :, own]
+    out = [None] + [remote(done, done, c_send.at[o], c_recv.at[o], to(o) * 2 + core) for o in range(1, chips)]
+    over = [remote(done, done, d_send.at[0], d_recv.at[0], partner)]
+    for o in range(1, chips):
+        out[o].start()
+    over[0].start()
+    for o in range(1, chips):
+        out[o].wait_recv()
+        piece = o_ref.at[frm(o), :, own]
+        over.append(remote(piece, piece, d_send.at[o], d_recv.at[o], partner))
+        over[o].start()
+    for o in range(chips):
+        over[o].wait_recv()
+    for o in range(chips):
+        halves[o].wait_send()
+        over[o].wait_send()
+        if o:
+            terms[o].wait_send()
+            out[o].wait_send()
+
+
+def added(x, term, cid):
+    chips, d = 8, x.shape[1]
+    blocks = (chips, x.shape[0] // chips, d)
+    share = (chips, blocks[1], d // 2)
+    sem = pltpu.SemaphoreType.DMA((chips,))
+    out = pl.pallas_call(
+        functools.partial(add_kernel, chips),
+        out_shape=jax.ShapeDtypeStruct(blocks, BF16),
+        in_specs=[pl.BlockSpec(memory_space=pltpu.VMEM)] * 2,
+        out_specs=pl.BlockSpec(memory_space=pltpu.VMEM),
+        scratch_shapes=[pltpu.VMEM(share, BF16)] * 3 + [sem] * 8,
+        compiler_params=pltpu.CompilerParams(collective_id=cid, has_side_effects=True),
+        name="added%d" % cid,
+    )(term.astype(BF16).reshape(blocks), x.reshape(blocks))
+    return out.reshape(x.shape)
+
+
 def solution(mesh):
-    def added(t, term):
-        return (t.astype(jnp.float32) + lax.psum(term.astype(jnp.bfloat16), "tp").astype(jnp.float32)).astype(jnp.bfloat16)
-
     def step(x, k_cache, v_cache, gain_a, wq, wo, gain_m, w_gate, w_up, w_down):
         seen = seen_by(normed(x, gain_a), wq, k_cache, v_cache, HEAD, THETA)
-        h = added(x, jnp.dot(seen, wo, preferred_element_type=jnp.float32))
-        return added(h, jnp.dot(hidden_of(normed(h, gain_m), w_gate, w_up), w_down, preferred_element_type=jnp.float32))
+        h = added(x, jnp.dot(seen, wo, preferred_element_type=jnp.float32), 0)
+        return added(h, jnp.dot(hidden_of(normed(h, gain_m), w_gate, w_up), w_down, preferred_element_type=jnp.float32), 1)
 
     states, cache, columns, rows_of = P("dp", None), P("dp", None, "tp", None), P(None, "tp"), P("tp", None)
     return jax.shard_map(

time: 285 us -> 138 us (0.48)
  waiting for transfers between devices: 185 us -> 0 us
  Pallas kernels: 0 us -> 50 us
  between operations: 13.6 us -> 0.21 us
    psum x2 -> x0, waiting for transfers between devices: 185 us -> none  [added(): lax.psum(term.astype(jnp.bfloat16), 'tp').astype(jnp.float32)]
    pallas_call x0 -> x2, Pallas kernels: none -> 50 us  [added(): pl.pallas_call(functools.partial(add_kernel, chips), out_shape=jax.ShapeD...]
  transfers between devices with their start and end apart: 2 -> 0, of which waited for: 2 -> 0; matrix products, arithmetic and copies ran while one was open for 0% -> 0% of each run, Pallas kernels for 0% -> 0%
where the time goes in v1:
time: 138 us; the launch traced here: 137 us
  matrix products  81.4 us (59%)
  Pallas kernels  50 us (36%)
  other arithmetic  3.59 us (3%)
  local copies, waits for them, and re-layouts  2.18 us (2%)
    pallas_call x2, Pallas kernels, added(): pl.pallas_call(functools.partial(add_kernel, chips), out_shape=jax.ShapeD...  50 us
    sub x1, matrix products, seen_by(): weights = jax.nn.softmax(scores, -1).astype(jnp.bfloat16)  27.1 us
    dot_general x1, matrix products, einsum(): return jnp.einsum(form, a.astype(jnp.float32), b.astype(jnp.float32))  23.3 us
    dot_general x1, matrix products, hidden_of(): gate = jnp.dot(b, w_gate, preferred_element_type=jnp.float32)  11.5 us
    dot_general x1, matrix products, hidden_of(): up = jnp.dot(b, w_up, preferred_element_type=jnp.float32)  11.1 us
    dot_general x1, matrix products, step(): jnp.dot(hidden_of(normed(h, gain_m), w_gate, w_up), w_down, preferred_ele...  4.59 us

profile of v1, /device:TPU:0, one launch (start us, length us, event | category | flops | bytes accessed | tf_op | source)
XLA Modules:
  0.0 137.4 jit_solution(8881473006809244234)
XLA Ops:
  0.0 0.9 convert_element_type.58
  0.9 1.3 fusion.13
  2.2 2.4 %convolution_convert_fusion.2 = bf16[64,256]{1,0:T(8,128)(2,1)S(1)} fusion(bf16[4608,256]{1,0:T(8,128)(2,1)} %param.14, bf16[64,4608]{1,0:T(8,128)(2,1)} %param.10, f32[4608]{0:T(1024)S(1)} %convert_element_type.58, f32[64]{0:T(128)S(1)} %add_rsqrt_fusion.1), kind=kOutput, calls=%fused_computation.27 | convolution fusion | flops 152190976 | bytes 3000576 | tf_op jit(solution)/shard_map/dot_general | solution.py:31
  4.6 0.1 fusion.39
  4.8 0.1 pad_maximum_fusion
  4.9 27.1 %fusion.40 = (f32[64,2]{1,0:T(8,128)S(1)}, f32[64,2,4096]{2,1,0:T(2,128)}) fusion(bf16[64,4096,1,128]{3,1,2,0:T(8,128)(2,1)} %param.11, bf16[64,2,128]{2,0,1:T(8,128)(2,1)S(1)} %pad_maximum_fusion), kind=kOutput, calls=%fused_computation.50 | convolution fusion | flops 135794688 | bytes 69239296 | tf_op jit(solution)/shard_map/sub | solution.py:43
  32.0 23.3 %fusion.20 = bf16[64,2,128]{2,1,0:T(2,128)(2,1)S(1)} fusion(bf16[64,4096,1,128]{3,1,2,0:T(8,128)(2,1)} %param.12, f32[64,2,4096]{2,1,0:T(2,128)} %get-tuple-element.10, f32[64,2]{1,0:T(8,128)S(1)} %get-tuple-element.9), kind=kOutput, calls=%fused_computation.26 | convolution fusion | flops 135282688 | bytes 69239296 | tf_op jit(solution)/shard_map/bgsu,bugd->bgsd/dot_general | solution.py:35
  55.4 0.0 copy-start.2
  55.4 1.4 fusion.5.t_ref
  56.7 25.5 %added0.1.x_ref = bf16[8,8,4608]{2,1,0:T(8,128)(2,1)} custom-call(bf16[8,8,4608]{2,1,0:T(8,128)(2,1)} %fusion.5.t_ref, bf16[8,8,4608]{2,1,0:T(8,128)(2,1)} %bitcast.40), custom_call_target="tpu_custom_call" | custom-call | tf_op jit(solution)/shard_map/added0/pallas_call | solution.py:117
  82.3 1.3 fusion.19
  83.6 0.1 rsqrt.21
  83.7 0.0 slice-start
  83.7 0.0 slice-start.1
  83.7 0.0 slice-start.2
  83.7 11.5 %fusion.28 = f32[64,2304]{1,0:T(8,128)S(1)} fusion(bf16[4608,2304]{1,0:T(8,128)(2,1)} %param.17, bf16[8,8,4608]{2,1,0:T(8,128)(2,1)} %added0.1.x_ref, f32[4608]{0:T(1024)S(1)} %convert_element_type.69, f32[64]{0:T(128)S(1)} %rsqrt.21), kind=kOutput, calls=%fused_computation.31 | convolution fusion | flops 1360134144 | bytes 22432000 | tf_op jit(solution)/shard_map/dot_general | solution.py:48
  95.2 0.0 slice-start.3
  95.2 0.0 slice-start.4
  95.2 0.0 slice-start.5
  95.2 11.1 %fusion.12 = bf16[64,2304]{1,0:T(8,128)(2,1)S(1)} fusion(bf16[4608,2304]{1,0:T(8,128)(2,1)} %param.18, f32[64,2304]{1,0:T(8,128)S(1)} %fusion.28, bf16[8,8,4608]{2,1,0:T(8,128)(2,1)S(1)} %copy-done.1, f32[4608]{0:T(1024)S(1)} %convert_element_type.69, f32[64]{0:T(128)S(1)} %rsqrt.21), kind=kOutput, calls=%fused_computation.13 | convolution fusion | flops 1361018880 | bytes 22726912 | tf_op jit(solution)/shard_map/dot_general | solution.py:49
  106.3 0.0 slice-done
  106.4 4.6 %fusion.6.t_ref = bf16[8,8,4608]{2,1,0:T(8,128)(2,1)} fusion(bf16[64,2304]{1,0:T(8,128)(2,1)S(1)} %fusion.12, bf16[2304,4608]{1,0:T(8,128)(2,1)S(1)} %bitcast.39), kind=kOutput, calls=%fused_computation.8 | convolution fusion | flops 1359249408 | bytes 22118400 | tf_op jit(solution)/shard_map/dot_general | solution.py:133
  111.0 24.5 %added1.1 = bf16[8,8,4608]{2,1,0:T(8,128)(2,1)} custom-call(bf16[8,8,4608]{2,1,0:T(8,128)(2,1)} %fusion.6.t_ref, bf16[8,8,4608]{2,1,0:T(8,128)(2,1)} %added0.1.x_ref), custom_call_target="tpu_custom_call" | custom-call | tf_op jit(solution)/shard_map/added1/pallas_call | solution.py:117
  135.5 1.9 %copy.31 = bf16[64,4608]{1,0:T(8,128)(2,1)} copy(bf16[64,4608]{1,0:T(8,128)(2,1)} %bitcast.41) | data formatting | bytes 1179648
  (17 shorter events, 0.1 us)
Async XLA Ops:
  0.0 55.4 %copy-start = (bf16[256,4608]{1,0:T(8,128)(2,1)S(1)}, bf16[256,4608]{1,0:T(8,128)(2,1)}, u32[]{:S(2)}) copy-start(bf16[256,4608]{1,0:T(8,128)(2,1)} %param.15) | copy-start | bytes 7077892
  55.4 28.3 %copy-start.2 = (bf16[4608]{0:T(1024)(128)(2,1)S(1)}, bf16[4608]{0:T(1024)(128)(2,1)}, u32[]{:S(2)}) copy-start(bf16[4608]{0:T(1024)(128)(2,1)} %param.16) | copy-start | bytes 27652
  83.7 11.5 %copy-start.1 = (bf16[8,8,4608]{2,1,0:T(8,128)(2,1)S(1)}, bf16[8,8,4608]{2,1,0:T(8,128)(2,1)}, u32[]{:S(2)}) copy-start(bf16[8,8,4608]{2,1,0:T(8,128)(2,1)} %added0.1.x_ref) | copy-start | bytes 1769476
  83.7 22.6 %slice-start = ((s8[21233664]{0:T(1024)(128)(4,1)}), s8[4194304]{0:T(1024)(128)(4,1)S(1)}, s32[]{:S(2)}) async-start(s8[21233664]{0:T(1024)(128)(4,1)} %bitcast.38), calls=%async_computation | async-start | bytes 8388608
  83.7 22.6 %slice-start.1 = ((s8[21233664]{0:T(1024)(128)(4,1)}), s8[4194304]{0:T(1024)(128)(4,1)S(1)}, s32[]{:S(2)}) async-start(s8[21233664]{0:T(1024)(128)(4,1)} %bitcast.38), calls=%async_computation.1 | async-start | bytes 8388608
  83.7 22.6 %slice-start.2 = ((s8[21233664]{0:T(1024)(128)(4,1)}), s8[4194304]{0:T(1024)(128)(4,1)S(1)}, s32[]{:S(2)}) async-start(s8[21233664]{0:T(1024)(128)(4,1)} %bitcast.38), calls=%async_computation.2 | async-start | bytes 8388608
  95.2 11.1 %slice-start.3 = ((s8[21233664]{0:T(1024)(128)(4,1)}), s8[4194304]{0:T(1024)(128)(4,1)S(1)}, s32[]{:S(2)}) async-start(s8[21233664]{0:T(1024)(128)(4,1)} %bitcast.38), calls=%async_computation.3 | async-start | bytes 8388608
  95.2 11.1 %slice-start.4 = ((s8[21233664]{0:T(1024)(128)(4,1)}), s8[4194304]{0:T(1024)(128)(4,1)S(1)}, s32[]{:S(2)}) async-start(s8[21233664]{0:T(1024)(128)(4,1)} %bitcast.38), calls=%async_computation.4 | async-start | bytes 8388608
  95.2 11.1 %slice-start.5 = ((s8[21233664]{0:T(1024)(128)(4,1)}), s8[262144]{0:T(1024)(128)(4,1)S(1)}, s32[]{:S(2)}) async-start(s8[21233664]{0:T(1024)(128)(4,1)} %bitcast.38), calls=%async_computation.5 | async-start | bytes 524288

commit v2 on v0

v2 whole, which is shorter than its diff:
```python
import functools

import jax
import jax.numpy as jnp
import numpy as np
from jax import lax
from jax.experimental import pallas as pl
from jax.experimental.pallas import tpu as pltpu
from jax.sharding import PartitionSpec as P

HEAD = 128
THETA = 10000
CHIPS = 8
MESH = pl.DeviceIdType.MESH
F32, BF16 = jnp.float32, jnp.bfloat16
NT = (((1,), (1,)), ((), ()))


def rotation(place):
    half = HEAD // 2
    step = np.float32(THETA) ** (-np.arange(half, dtype=np.float32) / np.float32(half))
    angle = (np.float32(place) * step).astype(np.float64)
    cos, sin = np.cos(angle), np.sin(angle)
    return np.stack([np.concatenate([cos, cos]), np.concatenate([-sin, sin])]).astype(np.float32)


class Sum:
    def __init__(self, t, residual, out, place, wide, bufs, sems, half):
        self.t, self.residual, self.out, self.place, self.wide = t, residual, out, place, wide
        self.r0, self.s1, self.r1 = bufs
        self.sems = sems
        self.half = half
        me = lax.axis_index("tp")
        self.core, self.chip = me % 2, me // 2
        self.partner = me + 1 - 2 * self.core

    def to(self, o):
        return (self.chip + o) % CHIPS

    def at(self, j, core):
        block, column = self.place(j)
        return block, slice(None), pl.ds(pl.multiple_of(core * self.half + column, 128), self.wide)

    def remote(self, src, dst, kind, o, device):
        return pltpu.make_async_remote_copy(
            src_ref=src, dst_ref=dst, send_sem=self.sems.at[kind, o], recv_sem=self.sems.at[kind + 1, o],
            device_id={"tp": device}, device_id_type=MESH,
        )

    def halves(self, o):
        return self.remote(self.t.at[self.at(self.to(o), 1 - self.core)], self.r0.at[o], 0, o, self.partner)

    def terms(self, o):
        return self.remote(self.s1.at[o], self.r1.at[o], 2, o, self.to(o) * 2 + self.core)

    def shares(self, o):
        done = self.out.at[self.at(self.chip, self.core)]
        return self.remote(done, done, 4, o, self.to(o) * 2 + self.core)

    def over(self, o):
        piece = self.out.at[self.at((self.chip + CHIPS - o) % CHIPS, self.core)]
        return self.remote(piece, piece, 6, o, self.partner)

    def send_halves(self):
        for o in [*range(1, CHIPS), 0]:
            self.halves(o).start()

    def send_terms(self):
        for o in range(1, CHIPS):
            self.halves(o).wait_recv()
            self.s1[o] = (self.t[self.at(self.to(o), self.core)].astype(F32) + self.r0[o].astype(F32)).astype(BF16)
            self.terms(o).start()

    def finish(self):
        self.halves(0).wait_recv()
        mine = self.at(self.chip, self.core)
        total = self.t[mine].astype(F32) + self.r0[0].astype(F32)
        for o in range(1, CHIPS):
            self.terms(o).wait_recv()
            total = total + self.r1[o].astype(F32)
        self.out[mine] = (self.residual[mine].astype(F32) + total).astype(BF16)
        for o in range(1, CHIPS):
            self.shares(o).start()
        self.over(0).start()

    def forward(self):
        for o in range(1, CHIPS):
            self.shares(o).wait_recv()
            self.over(o).start()

    def settle(self):
        for o in range(CHIPS):
            self.over(o).wait_recv()
        for o in range(CHIPS):
            self.halves(o).wait_send()
            self.over(o).wait_send()
            if o:
                self.terms(o).wait_send()
                self.shares(o).wait_send()


def layer_kernel(
    turn_ref, x_hbm, k_hbm, v_hbm, ga_hbm, wq_hbm, wo_hbm, gm_hbm, wg_hbm, wu_hbm, wd_hbm, o_ref,
    ring, wo, x3, h3, t3, rows16, hidden, q_ref, seen, s_ref, ga, gm,
    r0a, s1a, r1a, r0b, s1b, r1b, r0c, s1c, r1c,
    ring_sem, misc_sem, sem_a, sem_b, sem_c,
):
    d = x3.shape[2]
    half = d // 2
    cache = k_hbm.shape[1]
    ff = wg_hbm.shape[1]
    groups = x3.shape[0]
    me = lax.axis_index("tp")
    core, chip = me % 2, me // 2
    partner = me + 1 - 2 * core

    barrier = pltpu.get_barrier_semaphore()
    pl.semaphore_signal(barrier, inc=1, device_id={"tp": partner}, device_id_type=MESH)
    for o in range(1, CHIPS):
        pl.semaphore_signal(barrier, inc=1, device_id={"tp": (chip + o) % CHIPS * 2 + core}, device_id_type=MESH)

    def copy(src, dst, sem):
        return pltpu.make_async_copy(src, dst, sem)

    def cache_copy(g, i, j):
        src = k_hbm if i < 4 else v_hbm
        b = g * 8 + 2 * (i % 4) + j
        return copy(src.at[b], ring.at[g % 3, i, 0:cache, j * HEAD:(j + 1) * HEAD], ring_sem.at[g % 3, i, j])

    def fill(g, slots=range(8)):
        for i in slots:
            for j in range(2):
                cache_copy(g, i, j).start()

    def ffn_slot(f):
        return (groups + f // 8) % 3, f % 8

    def up_copy(f):
        src = (wg_hbm, wu_hbm)[f % 2]
        at = ffn_slot(f)
        return copy(src.at[:, (f // 2) * 256:(f // 2 + 1) * 256], ring.at[at], ring_sem.at[at[0], at[1], 0])

    def down_column(k):
        side = 1 - core if k < 9 else core
        return pl.multiple_of(side * half + (k % 9) * 256, 128)

    def down_copy(k):
        at = ffn_slot(18 + k // 2)
        return copy(wd_hbm.at[:, pl.ds(down_column(k), 256)], ring.at[at[0], at[1], (k % 2) * ff:(k % 2 + 1) * ff], ring_sem.at[at[0], at[1], k % 2])

    def fill_ffn(slots):
        for f in slots:
            if f < 18:
                up_copy(f).start()
            else:
                down_copy(2 * (f - 18)).start()
                down_copy(2 * (f - 18) + 1).start()

    x_copy = copy(x_hbm, x3, misc_sem.at[0])
    ga_copy = copy(ga_hbm, ga, misc_sem.at[1])
    wq_copy = copy(wq_hbm, ring.at[2, 7], ring_sem.at[2, 7, 0])
    wo_copy = copy(wo_hbm, wo, misc_sem.at[2])
    gm_copy = copy(gm_hbm, gm, misc_sem.at[3])
    x_copy.start()
    ga_copy.start()
    wq_copy.start()
    fill(0)
    fill(1)
    fill(2, range(7))
    wo_copy.start()
    gm_copy.start()

    def norm(src, gain):
        def pair(i, carry):
            wide = jnp.concatenate([src[2 * i], src[2 * i + 1]], axis=0).astype(F32)
            scale = lax.rsqrt(jnp.mean(wide * wide, -1, keepdims=True) + 1e-6)
            rows16[pl.ds(pl.multiple_of(16 * i, 16), 16), :] = (wide * scale * gain[...].astype(F32)).astype(BF16)
            return carry
        lax.fori_loop(0, groups // 2, pair, 0)

    x_copy.wait()
    ga_copy.wait()
    norm(x3, ga)
    wq_copy.wait()
    q = jnp.dot(rows16[...], ring[2, 7], preferred_element_type=F32).astype(BF16).astype(F32)
    fill(2, [7])
    turned = []
    for s in range(2):
        t = q[:, s * HEAD:(s + 1) * HEAD]
        turned.append(t * turn_ref[0:1, :] + pltpu.roll(t, HEAD // 2, 1) * turn_ref[1:2, :])
    for g in range(groups):
        q_ref[g] = jnp.concatenate([t[8 * g:8 * g + 8] for t in turned], axis=0).astype(BF16).astype(F32)
    wo_copy.wait()
    pl.semaphore_wait(barrier, CHIPS)

    def chunk_place(first):
        return lambda j: (first + j // 2, (j % 2) * (half // 2))

    sum_a = Sum(t3, x3, h3, chunk_place(0), half // 2, (r0a, s1a, r1a), sem_a, half)
    sum_b = Sum(t3, x3, h3, chunk_place(groups // 2), half // 2, (r0b, s1b, r1b), sem_b, half)
    sum_c = Sum(t3, h3, o_ref, lambda j: (j, 0), half, (r0c, s1c, r1c), sem_c, half)

    def attend(g):
        row = lax.broadcasted_iota(jnp.int32, (16, HEAD), 0) % 8
        base = g % 3
        q16 = q_ref[g]
        for i in range(4):
            for j in range(2):
                cache_copy(g, i, j).wait()
        lhs = [
            jnp.concatenate([jnp.where(row == 2 * p + j, q16, 0.0) for j in range(2)], axis=1).astype(BF16)
            for p in range(4)
        ]
        chunk = 512
        for c in range(0, cache, chunk):
            s = None
            for p in range(4):
                part = lax.dot_general(lhs[p], ring[base, p, c:c + chunk, :], NT, preferred_element_type=F32)
                s = part if s is None else s + part
            s_ref[:, c:c + chunk] = s
        s = s_ref[...] * HEAD**-0.5
        e = jnp.exp(s - jnp.max(s, -1, keepdims=True))
        w = (e * (1.0 / jnp.sum(e, -1, keepdims=True))).astype(BF16)
        for i in range(4, 8):
            for j in range(2):
                cache_copy(g, i, j).wait()
        acc = jnp.zeros((16, HEAD), F32)
        for p in range(4):
            got = jnp.dot(w, ring[base, 4 + p, 0:cache, :], preferred_element_type=F32)
            for j in range(2):
                acc = jnp.where(row == 2 * p + j, got[:, j * HEAD:(j + 1) * HEAD], acc)
        at = pl.ds(pl.multiple_of(8 * g, 8), 8)
        seen[at, 0:HEAD] = acc[0:8]
        seen[at, HEAD:] = acc[8:16]

    def project(first):
        count = groups // 2
        rows = seen[8 * first:8 * (first + count), :].astype(BF16)
        for c in range(0, d, 768):
            term = jnp.dot(rows, wo[:, c:c + 768], preferred_element_type=F32)
            for i in range(count):
                t3[first + i, :, c:c + 768] = term[8 * i:8 * i + 8].astype(BF16)

    def body(g, carry):
        attend(g)
        @pl.when(g < groups - 3)
        def _():
            fill(g + 3)
        for n in range(3):
            @pl.when(g == groups - 3 + n)
            def _():
                fill_ffn(range(8 * n, 8 * n + 8))
        @pl.when(g == groups // 2 - 1)
        def _():
            project(0)
            sum_a.send_halves()
        @pl.when(g == groups // 2)
        def _():
            sum_a.send_terms()
        @pl.when(g == groups // 2 + 1)
        def _():
            sum_a.finish()
        @pl.when(g == groups // 2 + 2)
        def _():
            sum_a.forward()
        return carry

    lax.fori_loop(0, groups, body, 0)
    project(groups // 2)
    sum_b.send_halves()
    sum_b.send_terms()
    sum_a.settle()
    sum_b.finish()
    sum_b.forward()
    gm_copy.wait()
    sum_b.settle()
    norm(h3, gm)

    for i in range(3):
        for f in range(6 * i, 6 * i + 6):
            up_copy(f).wait()
        for n in range(3 * i, 3 * i + 3):
            gate = jnp.dot(rows16[...], ring[ffn_slot(2 * n)], preferred_element_type=F32)
            up = jnp.dot(rows16[...], ring[ffn_slot(2 * n + 1)], preferred_element_type=F32)
            hidden[:, n * 256:(n + 1) * 256] = (jax.nn.silu(gate) * up).astype(BF16)
        if i == 0:
            fill_ffn(range(24, 27))

    def down(blocks):
        for k in blocks:
            down_copy(k).wait()
        for k in blocks:
            at = ffn_slot(18 + k // 2)
            term = jnp.dot(hidden[...], ring[at[0], at[1], (k % 2) * ff:(k % 2 + 1) * ff, :], preferred_element_type=F32)
            for i in range(groups):
                t3[i, :, pl.ds(down_column(k), 256)] = term[8 * i:8 * i + 8].astype(BF16)

    down(range(0, 9))
    sum_c.send_halves()
    down(range(9, 18))
    sum_c.send_terms()
    sum_c.finish()
    sum_c.forward()
    sum_c.settle()


def layer(x, k_cache, v_cache, gain_a, wq, wo, gain_m, w_gate, w_up, w_down):
    rows, d = x.shape
    cache = k_cache.shape[1]
    ff = w_gate.shape[1]
    blocks = (CHIPS, rows // CHIPS, d)
    wide = d // 4
    small, large = (CHIPS, 8, wide), (CHIPS, 8, 2 * wide)
    dma = pltpu.SemaphoreType.DMA
    anywhere = pl.BlockSpec(memory_space=pl.ANY)
    vmem = pl.BlockSpec(memory_space=pltpu.VMEM)
    scratch = [
        pltpu.VMEM((3, 8, d, 256), BF16),
        pltpu.VMEM(wo.shape, BF16),
        pltpu.VMEM(blocks, BF16),
        pltpu.VMEM(blocks, BF16),
        pltpu.VMEM(blocks, BF16),
        pltpu.VMEM((rows, d), BF16),
        pltpu.VMEM((rows, ff), BF16),
        pltpu.VMEM((rows // 8, 16, HEAD), F32),
        pltpu.VMEM((rows, 2 * HEAD), F32),
        pltpu.VMEM((16, cache), F32),
        pltpu.VMEM((1, d), BF16),
        pltpu.VMEM((1, d), BF16),
    ]
    scratch += [pltpu.VMEM(small, BF16)] * 6 + [pltpu.VMEM(large, BF16)] * 3
    scratch += [dma((3, 8, 2)), dma((4,))] + [dma((8, CHIPS))] * 3
    out = pl.pallas_call(
        layer_kernel,
        out_shape=jax.ShapeDtypeStruct(blocks, BF16),
        in_specs=[vmem] + [anywhere] * 10,
        out_specs=vmem,
        scratch_shapes=scratch,
        compiler_params=pltpu.CompilerParams(collective_id=0, has_side_effects=True, vmem_limit_bytes=66_200_000),
        name="layer",
    )(
        jnp.asarray(rotation(cache - 1)), x.reshape(blocks), k_cache.reshape(rows, cache, HEAD), v_cache.reshape(rows, cache, HEAD),
        gain_a.reshape(1, d), wq, wo, gain_m.reshape(1, d), w_gate, w_up, w_down,
    )
    return out.reshape(x.shape)


def solution(mesh):
    states, cache, columns, rows_of = P("dp", None), P("dp", None, "tp", None), P(None, "tp"), P("tp", None)
    return jax.shard_map(
        layer,
        mesh=mesh,
        in_specs=(states, cache, cache, P(None), columns, rows_of, P(None), columns, columns, rows_of),
        out_specs=states,
        check_vma=False,
    )
```

time: 285 us -> 104 us (0.36)
  waiting for transfers between devices: 185 us -> 0 us
  Pallas kernels: 0 us -> 99.6 us
  matrix products: 79.5 us -> 0 us
  between operations: 13.6 us -> 0.01 us
  other arithmetic: 6.3 us -> 0 us
  local copies, waits for them, and re-layouts: 0.18 us -> 4.54 us
    psum x2 -> x0, waiting for transfers between devices: 185 us -> none  [added(): lax.psum(term.astype(jnp.bfloat16), 'tp').astype(jnp.float32)]
    pallas_call x0 -> x1, Pallas kernels: none -> 99.6 us  [layer(): pl.pallas_call(layer_kernel, out_shape=jax.ShapeDtypeStruct(blocks, BF16)...]
    dot_general x6 -> x0, matrix products: 52.3 us -> none  [the longest x1 23.3 us: einsum(): return jnp.einsum(form, a.astype(jnp.float32), b.astype(jnp.float32))]
    sub x1 -> x0, matrix products: 27.1 us -> none  [seen_by(): weights = jax.nn.softmax(scores, -1).astype(jnp.bfloat16)]
    convert_element_type x3 -> x0, other arithmetic: 3.47 us -> none  [the longest x1 2.01 us: added(): (t.astype(jnp.float32) + lax.psum(term.astype(jnp.bfloat16), 'tp').astype...]
  transfers between devices with their start and end apart: 2 -> 0, of which waited for: 2 -> 0; matrix products, arithmetic and copies ran while one was open for 0% -> 0% of each run, Pallas kernels for 0% -> 0%
where the time goes in v2:
time: 104 us
  Pallas kernels  99.6 us (96%)
  local copies, waits for them, and re-layouts  4.54 us (4%)
    pallas_call x1, Pallas kernels, layer(): pl.pallas_call(layer_kernel, out_shape=jax.ShapeDtypeStruct(blocks, BF16)...  99.6 us

profile of v2, /device:TPU:0, one launch (start us, length us, event | category | flops | bytes accessed | tf_op | source)
XLA Modules:
  0.0 104.1 jit_solution(8602853370971482336)
XLA Ops:
  0.0 1.3 %reshape.21.ga_hbm = bf16[1,4608]{1,0:T(2,128)(2,1)} reshape(bf16[4608]{0:T(1024)(128)(2,1)} %param.14) | data formatting | bytes 18432 | tf_op jit(solution)/shard_map/reshape | solution.py:343
  1.3 1.3 %reshape.22.gm_hbm = bf16[1,4608]{1,0:T(2,128)(2,1)} reshape(bf16[4608]{0:T(1024)(128)(2,1)} %param.17) | data formatting | bytes 18432 | tf_op jit(solution)/shard_map/reshape | solution.py:343
  2.6 99.6 %layer.1 = bf16[8,8,4608]{2,1,0:T(8,128)(2,1)} custom-call(f32[2,128]{1,0:T(2,128)} %constant.2.clone.turn_ref, bf16[8,8,4608]{2,1,0:T(8,128)(2,1)} %bitcast.5, bf16[64,4096,128]{2,1,0:T(8,128)(2,1)} %bitcast.1.k_hbm, bf16[64,4096,128]{2,1,0:T(8,128)(2,1)} %bitcast.2.v_hbm, bf16[1,4608]{1,0:T(2,128)(2,1)} %reshape.21.ga_hbm, bf16[4608,256]{1,0:T(8,128)(2,1)} %wq_hbm.1, ...), custom_call_target="tpu_custom_call" | custom-call | tf_op jit(solution)/shard_map/layer/pallas_call | solution.py:333
  102.2 1.9 %copy.13 = bf16[64,4608]{1,0:T(8,128)(2,1)} copy(bf16[64,4608]{1,0:T(8,128)(2,1)} %bitcast.4) | data formatting | bytes 1179648

commit v3 on v2

--- a/solution.py
+++ b/solution.py
@@ -11,6 +11,8 @@
 HEAD = 128
 THETA = 10000
 CHIPS = 8
+PARTS = 3
+KEYS, VALUES = range(4), range(4, 8)
 MESH = pl.DeviceIdType.MESH
 F32, BF16 = jnp.float32, jnp.bfloat16
 NT = (((1,), (1,)), ((), ()))
@@ -141,8 +143,8 @@
         return copy(src.at[:, (f // 2) * 256:(f // 2 + 1) * 256], ring.at[at], ring_sem.at[at[0], at[1], 0])
 
     def down_column(k):
-        side = 1 - core if k < 9 else core
-        return pl.multiple_of(side * half + (k % 9) * 256, 128)
+        side = core if k % 6 >= 3 else 1 - core
+        return pl.multiple_of(side * half + k // 6 * (half // PARTS) + k % 3 * 256, 128)
 
     def down_copy(k):
         at = ffn_slot(18 + k // 2)
@@ -164,26 +166,24 @@
     x_copy.start()
     ga_copy.start()
     wq_copy.start()
-    fill(0)
-    fill(1)
-    fill(2, range(7))
-    wo_copy.start()
-    gm_copy.start()
+    fill(0, KEYS)
 
     def norm(src, gain):
         def pair(i, carry):
             wide = jnp.concatenate([src[2 * i], src[2 * i + 1]], axis=0).astype(F32)
             scale = lax.rsqrt(jnp.mean(wide * wide, -1, keepdims=True) + 1e-6)
-            rows16[pl.ds(pl.multiple_of(16 * i, 16), 16), :] = (wide * scale * gain[...].astype(F32)).astype(BF16)
+            rows16[pl.ds(pl.multiple_of(16 * i, 16), 16), :] = (wide * scale * gain[...].astype(F32)[None, :]).astype(BF16)
             return carry
         lax.fori_loop(0, groups // 2, pair, 0)
 
     x_copy.wait()
     ga_copy.wait()
     norm(x3, ga)
+    fill(0, VALUES)
+    wo_copy.start()
+    gm_copy.start()
     wq_copy.wait()
     q = jnp.dot(rows16[...], ring[2, 7], preferred_element_type=F32).astype(BF16).astype(F32)
-    fill(2, [7])
     turned = []
     for s in range(2):
         t = q[:, s * HEAD:(s + 1) * HEAD]
@@ -193,12 +193,20 @@
     wo_copy.wait()
     pl.semaphore_wait(barrier, CHIPS)
 
-    def chunk_place(first):
-        return lambda j: (first + j // 2, (j % 2) * (half // 2))
-
-    sum_a = Sum(t3, x3, h3, chunk_place(0), half // 2, (r0a, s1a, r1a), sem_a, half)
-    sum_b = Sum(t3, x3, h3, chunk_place(groups // 2), half // 2, (r0b, s1b, r1b), sem_b, half)
-    sum_c = Sum(t3, h3, o_ref, lambda j: (j, 0), half, (r0c, s1c, r1c), sem_c, half)
+    def chunk_place(first, column):
+        return lambda j: (first + j // 2, (j % 2) * (half // 2) + column)
+
+    def bufs(*args):
+        return [buf.at[args[-1]] for buf in args[:-1]]
+
+    sum_a = Sum(t3, x3, h3, chunk_place(0, 0), half // 2, bufs(r0a, s1a, r1a, 0), sem_a.at[0], half)
+    sums_b = [
+        Sum(t3, x3, h3, chunk_place(groups // 2, n * (half // 2 // PARTS)), half // 2 // PARTS, bufs(r0b, s1b, r1b, n), sem_b.at[n], half)
+        for n in range(PARTS)
+    ]
+    sums_c = [
+        Sum(t3, h3, o_ref, lambda j, n=n: (j, n * (half // PARTS)), half // PARTS, bufs(r0c, s1c, r1c, n), sem_c.at[n], half) for n in range(PARTS)
+    ]
 
     def attend(g):
         row = lax.broadcasted_iota(jnp.int32, (16, HEAD), 0) % 8
@@ -207,6 +215,9 @@
         for i in range(4):
             for j in range(2):
                 cache_copy(g, i, j).wait()
+        @pl.when(g < groups - 1)
+        def _():
+            fill(g + 1, KEYS)
         lhs = [
             jnp.concatenate([jnp.where(row == 2 * p + j, q16, 0.0) for j in range(2)], axis=1).astype(BF16)
             for p in range(4)
@@ -224,6 +235,12 @@
         for i in range(4, 8):
             for j in range(2):
                 cache_copy(g, i, j).wait()
+        @pl.when(g < groups - 1)
+        def _():
+            fill(g + 1, VALUES)
+        @pl.when(g == groups - 1)
+        def _():
+            fill_ffn(range(8))
         acc = jnp.zeros((16, HEAD), F32)
         for p in range(4):
             got = jnp.dot(w, ring[base, 4 + p, 0:cache, :], preferred_element_type=F32)
@@ -243,13 +260,6 @@
 
     def body(g, carry):
         attend(g)
-        @pl.when(g < groups - 3)
-        def _():
-            fill(g + 3)
-        for n in range(3):
-            @pl.when(g == groups - 3 + n)
-            def _():
-                fill_ffn(range(8 * n, 8 * n + 8))
         @pl.when(g == groups // 2 - 1)
         def _():
             project(0)
@@ -267,13 +277,21 @@
 
     lax.fori_loop(0, groups, body, 0)
     project(groups // 2)
-    sum_b.send_halves()
-    sum_b.send_terms()
+    for b in sums_b:
+        b.send_halves()
+    for b in sums_b:
+        b.send_terms()
+    fill_ffn(range(8, 12))
     sum_a.settle()
-    sum_b.finish()
-    sum_b.forward()
+    for b in sums_b:
+        b.finish()
+    fill_ffn(range(12, 20))
+    for b in sums_b:
+        b.forward()
     gm_copy.wait()
-    sum_b.settle()
+    for b in sums_b:
+        b.settle()
+    fill_ffn(range(20, 24))
     norm(h3, gm)
 
     for i in range(3):
@@ -295,13 +313,27 @@
             for i in range(groups):
                 t3[i, :, pl.ds(down_column(k), 256)] = term[8 * i:8 * i + 8].astype(BF16)
 
-    down(range(0, 9))
-    sum_c.send_halves()
-    down(range(9, 18))
-    sum_c.send_terms()
-    sum_c.finish()
-    sum_c.forward()
-    sum_c.settle()
+    c0, c1, c2 = sums_c
+    down(range(0, 3))
+    c0.send_halves()
+    down(range(3, 6))
+    down(range(6, 9))
+    c1.send_halves()
+    c0.send_terms()
+    down(range(9, 12))
+    down(range(12, 15))
+    c2.send_halves()
+    c1.send_terms()
+    down(range(15, 18))
+    c2.send_terms()
+    c0.finish()
+    c1.finish()
+    c0.forward()
+    c2.finish()
+    c1.forward()
+    c2.forward()
+    for c in sums_c:
+        c.settle()
 
 
 def layer(x, k_cache, v_cache, gain_a, wq, wo, gain_m, w_gate, w_up, w_down):
@@ -310,7 +342,7 @@
     ff = w_gate.shape[1]
     blocks = (CHIPS, rows // CHIPS, d)
     wide = d // 4
-    small, large = (CHIPS, 8, wide), (CHIPS, 8, 2 * wide)
+    whole, small, large = (1, CHIPS, 8, wide), (PARTS, CHIPS, 8, wide // PARTS), (PARTS, CHIPS, 8, 2 * wide // PARTS)
     dma = pltpu.SemaphoreType.DMA
     anywhere = pl.BlockSpec(memory_space=pl.ANY)
     vmem = pl.BlockSpec(memory_space=pltpu.VMEM)
@@ -325,11 +357,11 @@
         pltpu.VMEM((rows // 8, 16, HEAD), F32),
         pltpu.VMEM((rows, 2 * HEAD), F32),
         pltpu.VMEM((16, cache), F32),
-        pltpu.VMEM((1, d), BF16),
-        pltpu.VMEM((1, d), BF16),
+        pltpu.VMEM((d,), BF16),
+        pltpu.VMEM((d,), BF16),
     ]
-    scratch += [pltpu.VMEM(small, BF16)] * 6 + [pltpu.VMEM(large, BF16)] * 3
-    scratch += [dma((3, 8, 2)), dma((4,))] + [dma((8, CHIPS))] * 3
+    scratch += [pltpu.VMEM(whole, BF16)] * 3 + [pltpu.VMEM(small, BF16)] * 3 + [pltpu.VMEM(large, BF16)] * 3
+    scratch += [dma((3, 8, 2)), dma((4,))] + [dma((1, 8, CHIPS))] + [dma((PARTS, 8, CHIPS))] * 2
     out = pl.pallas_call(
         layer_kernel,
         out_shape=jax.ShapeDtypeStruct(blocks, BF16),
@@ -340,7 +372,7 @@
         name="layer",
     )(
         jnp.asarray(rotation(cache - 1)), x.reshape(blocks), k_cache.reshape(rows, cache, HEAD), v_cache.reshape(rows, cache, HEAD),
-        gain_a.reshape(1, d), wq, wo, gain_m.reshape(1, d), w_gate, w_up, w_down,
+        gain_a, wq, wo, gain_m, w_gate, w_up, w_down,
     )
     return out.reshape(x.shape)
 

time: 104 us -> 96.4 us (0.927)
  Pallas kernels: 99.6 us -> 94.3 us
  local copies, waits for them, and re-layouts: 4.54 us -> 1.92 us
    pallas_call x1, Pallas kernels: 99.6 us -> 94.3 us  [layer(): pl.pallas_call(layer_kernel, out_shape=jax.ShapeDtypeStruct(blocks, BF16)...]
    reshape x2 -> x0, local copies, waits for them, and re-layouts: 2.63 us -> none  [the longest x1 1.32 us: layer(): gain_a.reshape(1, d)]
where the time goes in v3:
time: 96.4 us; the launch traced here: 96.3 us
  Pallas kernels  94.3 us (98%)
  local copies, waits for them, and re-layouts  1.92 us (2%)
    pallas_call x1, Pallas kernels, layer(): pl.pallas_call(layer_kernel, out_shape=jax.ShapeDtypeStruct(blocks, BF16)...  94.3 us

profile of v3, /device:TPU:0, one launch (start us, length us, event | category | flops | bytes accessed | tf_op | source)
XLA Modules:
  0.0 96.3 jit_solution(17329225679177858753)
XLA Ops:
  0.0 94.3 %layer.1 = bf16[8,8,4608]{2,1,0:T(8,128)(2,1)} custom-call(f32[2,128]{1,0:T(2,128)} %constant.2.clone.turn_ref, bf16[8,8,4608]{2,1,0:T(8,128)(2,1)} %bitcast.5, bf16[64,4096,128]{2,1,0:T(8,128)(2,1)} %bitcast.1.k_hbm, bf16[64,4096,128]{2,1,0:T(8,128)(2,1)} %bitcast.2.v_hbm, bf16[4608]{0:T(1024)(128)(2,1)} %ga_hbm.1, bf16[4608,256]{1,0:T(8,128)(2,1)} %wq_hbm.1, ...), custom_call_target="tpu_custom_call" | custom-call | tf_op jit(solution)/shard_map/layer/pallas_call | solution.py:365
  94.3 1.9 %copy.13 = bf16[64,4608]{1,0:T(8,128)(2,1)} copy(bf16[64,4608]{1,0:T(8,128)(2,1)} %bitcast.4) | data formatting | bytes 1179648

commit v4 on v3

--- a/solution.py
+++ b/solution.py
@@ -27,11 +27,10 @@
 
 
 class Sum:
-    def __init__(self, t, residual, out, place, wide, bufs, sems, half):
-        self.t, self.residual, self.out, self.place, self.wide = t, residual, out, place, wide
+    def __init__(self, t, residual, out, place, wide, bufs, sems, owners=CHIPS):
+        self.t, self.residual, self.out, self.place, self.wide, self.owners = t, residual, out, place, wide, owners
         self.r0, self.s1, self.r1 = bufs
         self.sems = sems
-        self.half = half
         me = lax.axis_index("tp")
         self.core, self.chip = me % 2, me // 2
         self.partner = me + 1 - 2 * self.core
@@ -39,9 +38,18 @@
     def to(self, o):
         return (self.chip + o) % CHIPS
 
+    def frm(self, o):
+        return (self.chip + CHIPS - o) % CHIPS
+
     def at(self, j, core):
-        block, column = self.place(j)
-        return block, slice(None), pl.ds(pl.multiple_of(core * self.half + column, 128), self.wide)
+        block, column = self.place(j, core)
+        return block, slice(None), pl.ds(pl.multiple_of(column, 128), self.wide)
+
+    def owned(self, j, act):
+        if self.owners == CHIPS:
+            act()
+        else:
+            pl.when(j < self.owners)(act)
 
     def remote(self, src, dst, kind, o, device):
         return pltpu.make_async_remote_copy(
@@ -55,50 +63,61 @@
     def terms(self, o):
         return self.remote(self.s1.at[o], self.r1.at[o], 2, o, self.to(o) * 2 + self.core)
 
-    def shares(self, o):
-        done = self.out.at[self.at(self.chip, self.core)]
+    def shares(self, o, chip):
+        done = self.out.at[self.at(chip, self.core)]
         return self.remote(done, done, 4, o, self.to(o) * 2 + self.core)
 
     def over(self, o):
-        piece = self.out.at[self.at((self.chip + CHIPS - o) % CHIPS, self.core)]
+        piece = self.out.at[self.at(self.frm(o), self.core)]
         return self.remote(piece, piece, 6, o, self.partner)
 
     def send_halves(self):
         for o in [*range(1, CHIPS), 0]:
-            self.halves(o).start()
+            self.owned(self.to(o), lambda o=o: self.halves(o).start())
 
     def send_terms(self):
-        for o in range(1, CHIPS):
+        def send(o):
             self.halves(o).wait_recv()
             self.s1[o] = (self.t[self.at(self.to(o), self.core)].astype(F32) + self.r0[o].astype(F32)).astype(BF16)
             self.terms(o).start()
 
+        for o in range(1, CHIPS):
+            self.owned(self.to(o), lambda o=o: send(o))
+
     def finish(self):
-        self.halves(0).wait_recv()
-        mine = self.at(self.chip, self.core)
-        total = self.t[mine].astype(F32) + self.r0[0].astype(F32)
+        def act():
+            self.halves(0).wait_recv()
+            mine = self.at(self.chip, self.core)
+            total = self.t[mine].astype(F32) + self.r0[0].astype(F32)
+            for o in range(1, CHIPS):
+                self.terms(o).wait_recv()
+                total = total + self.r1[o].astype(F32)
+            self.out[mine] = (self.residual[mine].astype(F32) + total).astype(BF16)
+            for o in range(1, CHIPS):
+                self.shares(o, self.chip).start()
+            self.over(0).start()
+
+        self.owned(self.chip, act)
+
+    def forward(self):
+        def act(o):
+            self.shares(o, self.frm(o)).wait_recv()
+            self.over(o).start()
+
         for o in range(1, CHIPS):
-            self.terms(o).wait_recv()
-            total = total + self.r1[o].astype(F32)
-        self.out[mine] = (self.residual[mine].astype(F32) + total).astype(BF16)
-        for o in range(1, CHIPS):
-            self.shares(o).start()
-        self.over(0).start()
-
-    def forward(self):
-        for o in range(1, CHIPS):
-            self.shares(o).wait_recv()
-            self.over(o).start()
+            self.owned(self.frm(o), lambda o=o: act(o))
 
     def settle(self):
         for o in range(CHIPS):
-            self.over(o).wait_recv()
+            self.owned(self.frm(o), lambda o=o: self.over(o).wait_recv())
+
+    def sent(self):
         for o in range(CHIPS):
-            self.halves(o).wait_send()
-            self.over(o).wait_send()
+            self.owned(self.to(o), lambda o=o: self.halves(o).wait_send())
+            self.owned(self.frm(o), lambda o=o: self.over(o).wait_send())
             if o:
-                self.terms(o).wait_send()
-                self.shares(o).wait_send()
+                self.owned(self.to(o), lambda o=o: self.terms(o).wait_send())
+                self.owned(self.chip, lambda o=o: self.shares(o, self.chip).wait_send())
 
 
 def layer_kernel(
@@ -166,20 +185,19 @@
     x_copy.start()
     ga_copy.start()
     wq_copy.start()
-    fill(0, KEYS)
-
-    def norm(src, gain):
+    fill(0)
+
+    def norm(src, gain, first, count):
         def pair(i, carry):
             wide = jnp.concatenate([src[2 * i], src[2 * i + 1]], axis=0).astype(F32)
             scale = lax.rsqrt(jnp.mean(wide * wide, -1, keepdims=True) + 1e-6)
             rows16[pl.ds(pl.multiple_of(16 * i, 16), 16), :] = (wide * scale * gain[...].astype(F32)[None, :]).astype(BF16)
             return carry
-        lax.fori_loop(0, groups // 2, pair, 0)
+        lax.fori_loop(first, first + count, pair, 0)
 
     x_copy.wait()
     ga_copy.wait()
-    norm(x3, ga)
-    fill(0, VALUES)
+    norm(x3, ga, 0, groups // 2)
     wo_copy.start()
     gm_copy.start()
     wq_copy.wait()
@@ -193,19 +211,16 @@
     wo_copy.wait()
     pl.semaphore_wait(barrier, CHIPS)
 
-    def chunk_place(first, column):
-        return lambda j: (first + j // 2, (j % 2) * (half // 2) + column)
-
     def bufs(*args):
         return [buf.at[args[-1]] for buf in args[:-1]]
 
-    sum_a = Sum(t3, x3, h3, chunk_place(0, 0), half // 2, bufs(r0a, s1a, r1a, 0), sem_a.at[0], half)
-    sums_b = [
-        Sum(t3, x3, h3, chunk_place(groups // 2, n * (half // 2 // PARTS)), half // 2 // PARTS, bufs(r0b, s1b, r1b, n), sem_b.at[n], half)
-        for n in range(PARTS)
+    block = half // PARTS
+    sum_a = Sum(t3, x3, h3, lambda j, c: (j // 2, c * half + (j % 2) * (half // 2)), half // 2, bufs(r0a, s1a, r1a, 0), sem_a.at[0])
+    sum_b, sum_d = [
+        Sum(t3, x3, h3, lambda j, c, n=n: (4 + 2 * n + c, j * block), block, bufs(r0b, s1b, r1b, n), sem_b.at[n], 2 * PARTS) for n in range(2)
     ]
     sums_c = [
-        Sum(t3, h3, o_ref, lambda j, n=n: (j, n * (half // PARTS)), half // PARTS, bufs(r0c, s1c, r1c, n), sem_c.at[n], half) for n in range(PARTS)
+        Sum(t3, h3, o_ref, lambda j, c, n=n: (j, c * half + n * block), block, bufs(r0c, s1c, r1c, n), sem_c.at[n]) for n in range(PARTS)
     ]
 
     def attend(g):
@@ -250,8 +265,7 @@
         seen[at, 0:HEAD] = acc[0:8]
         seen[at, HEAD:] = acc[8:16]
 
-    def project(first):
-        count = groups // 2
+    def project(first, count):
         rows = seen[8 * first:8 * (first + count), :].astype(BF16)
         for c in range(0, d, 768):
             term = jnp.dot(rows, wo[:, c:c + 768], preferred_element_type=F32)
@@ -260,40 +274,47 @@
 
     def body(g, carry):
         attend(g)
-        @pl.when(g == groups // 2 - 1)
-        def _():
-            project(0)
+        @pl.when(g == 3)
+        def _():
+            project(0, 4)
             sum_a.send_halves()
-        @pl.when(g == groups // 2)
+        @pl.when(g == 4)
         def _():
             sum_a.send_terms()
-        @pl.when(g == groups // 2 + 1)
-        def _():
+        @pl.when(g == 5)
+        def _():
+            project(4, 2)
+            sum_b.send_halves()
             sum_a.finish()
-        @pl.when(g == groups // 2 + 2)
-        def _():
+        @pl.when(g == 6)
+        def _():
+            sum_b.send_terms()
             sum_a.forward()
+        @pl.when(g == 7)
+        def _():
+            sum_b.finish()
         return carry
 
     lax.fori_loop(0, groups, body, 0)
-    project(groups // 2)
-    for b in sums_b:
-        b.send_halves()
-    for b in sums_b:
-        b.send_terms()
-    fill_ffn(range(8, 12))
+    project(6, 2)
+    sum_d.send_halves()
+    fill_ffn(range(8, 16))
+    sum_b.forward()
+    sum_d.send_terms()
+    gm_copy.wait()
     sum_a.settle()
-    for b in sums_b:
-        b.finish()
-    fill_ffn(range(12, 20))
-    for b in sums_b:
-        b.forward()
-    gm_copy.wait()
-    for b in sums_b:
-        b.settle()
-    fill_ffn(range(20, 24))
-    norm(h3, gm)
-
+    norm(h3, gm, 0, 2)
+    sum_d.finish()
+    fill_ffn(range(16, 24))
+    sum_b.settle()
+    norm(h3, gm, 2, 1)
+    sum_d.forward()
+    sum_a.sent()
+    sum_b.sent()
+    sum_d.settle()
+    norm(h3, gm, 3, 1)
+
+    sum_d.sent()
     for i in range(3):
         for f in range(6 * i, 6 * i + 6):
             up_copy(f).wait()
@@ -334,6 +355,7 @@
     c2.forward()
     for c in sums_c:
         c.settle()
+        c.sent()
 
 
 def layer(x, k_cache, v_cache, gain_a, wq, wo, gain_m, w_gate, w_up, w_down):
@@ -342,7 +364,7 @@
     ff = w_gate.shape[1]
     blocks = (CHIPS, rows // CHIPS, d)
     wide = d // 4
-    whole, small, large = (1, CHIPS, 8, wide), (PARTS, CHIPS, 8, wide // PARTS), (PARTS, CHIPS, 8, 2 * wide // PARTS)
+    whole, small, large = (1, CHIPS, 8, wide), (2, CHIPS, 8, 2 * wide // PARTS), (PARTS, CHIPS, 8, 2 * wide // PARTS)
     dma = pltpu.SemaphoreType.DMA
     anywhere = pl.BlockSpec(memory_space=pl.ANY)
     vmem = pl.BlockSpec(memory_space=pltpu.VMEM)
@@ -361,7 +383,7 @@
         pltpu.VMEM((d,), BF16),
     ]
     scratch += [pltpu.VMEM(whole, BF16)] * 3 + [pltpu.VMEM(small, BF16)] * 3 + [pltpu.VMEM(large, BF16)] * 3
-    scratch += [dma((3, 8, 2)), dma((4,))] + [dma((1, 8, CHIPS))] + [dma((PARTS, 8, CHIPS))] * 2
+    scratch += [dma((3, 8, 2)), dma((4,))] + [dma((1, 8, CHIPS))] + [dma((2, 8, CHIPS)), dma((PARTS, 8, CHIPS))]
     out = pl.pallas_call(
         layer_kernel,
         out_shape=jax.ShapeDtypeStruct(blocks, BF16),

time: 96.4 us -> 96.7 us (level)
  no operation moved by 1% of the time
where the time goes in v4:
time: 96.7 us; the launch traced here: 96.5 us
  Pallas kernels  94.6 us (98%)
  local copies, waits for them, and re-layouts  1.92 us (2%)
    pallas_call x1, Pallas kernels, layer(): pl.pallas_call(layer_kernel, out_shape=jax.ShapeDtypeStruct(blocks, BF16)...  94.6 us

profile of v4, /device:TPU:0, one launch (start us, length us, event | category | flops | bytes accessed | tf_op | source)
XLA Modules:
  0.0 96.5 jit_solution(4888118021991367212)
XLA Ops:
  0.0 94.6 %layer.1 = bf16[8,8,4608]{2,1,0:T(8,128)(2,1)} custom-call(f32[2,128]{1,0:T(2,128)} %constant.2.clone.turn_ref, bf16[8,8,4608]{2,1,0:T(8,128)(2,1)} %bitcast.5, bf16[64,4096,128]{2,1,0:T(8,128)(2,1)} %bitcast.1.k_hbm, bf16[64,4096,128]{2,1,0:T(8,128)(2,1)} %bitcast.2.v_hbm, bf16[4608]{0:T(1024)(128)(2,1)} %ga_hbm.1, bf16[4608,256]{1,0:T(8,128)(2,1)} %wq_hbm.1, ...), custom_call_target="tpu_custom_call" | custom-call | tf_op jit(solution)/shard_map/layer/pallas_call | solution.py:387
  94.6 1.9 %copy.13 = bf16[64,4608]{1,0:T(8,128)(2,1)} copy(bf16[64,4608]{1,0:T(8,128)(2,1)} %bitcast.4) | data formatting | bytes 1179648

commit v5 on v4

--- a/solution.py
+++ b/solution.py
@@ -215,9 +215,9 @@
         return [buf.at[args[-1]] for buf in args[:-1]]
 
     block = half // PARTS
-    sum_a = Sum(t3, x3, h3, lambda j, c: (j // 2, c * half + (j % 2) * (half // 2)), half // 2, bufs(r0a, s1a, r1a, 0), sem_a.at[0])
-    sum_b, sum_d = [
-        Sum(t3, x3, h3, lambda j, c, n=n: (4 + 2 * n + c, j * block), block, bufs(r0b, s1b, r1b, n), sem_b.at[n], 2 * PARTS) for n in range(2)
+    sum_a, sum_b = [
+        Sum(t3, x3, h3, lambda j, c, n=n: (4 * n + j // 2, c * half + (j % 2) * (half // 2)), half // 2, share, sems.at[0])
+        for n, (share, sems) in enumerate([(bufs(r0a, s1a, r1a, 0), sem_a), (bufs(r0b, s1b, r1b, 0), sem_b)])
     ]
     sums_c = [
         Sum(t3, h3, o_ref, lambda j, c, n=n: (j, c * half + n * block), block, bufs(r0c, s1c, r1c, n), sem_c.at[n]) for n in range(PARTS)
@@ -283,38 +283,27 @@
             sum_a.send_terms()
         @pl.when(g == 5)
         def _():
-            project(4, 2)
-            sum_b.send_halves()
             sum_a.finish()
         @pl.when(g == 6)
         def _():
-            sum_b.send_terms()
             sum_a.forward()
-        @pl.when(g == 7)
-        def _():
-            sum_b.finish()
         return carry
 
     lax.fori_loop(0, groups, body, 0)
-    project(6, 2)
-    sum_d.send_halves()
+    project(4, 4)
+    sum_b.send_halves()
     fill_ffn(range(8, 16))
-    sum_b.forward()
-    sum_d.send_terms()
+    sum_b.send_terms()
     gm_copy.wait()
     sum_a.settle()
     norm(h3, gm, 0, 2)
-    sum_d.finish()
+    sum_b.finish()
     fill_ffn(range(16, 24))
+    sum_a.sent()
+    sum_b.forward()
     sum_b.settle()
-    norm(h3, gm, 2, 1)
-    sum_d.forward()
-    sum_a.sent()
+    norm(h3, gm, 2, 2)
     sum_b.sent()
-    sum_d.settle()
-    norm(h3, gm, 3, 1)
-
-    sum_d.sent()
     for i in range(3):
         for f in range(6 * i, 6 * i + 6):
             up_copy(f).wait()
@@ -364,7 +353,7 @@
     ff = w_gate.shape[1]
     blocks = (CHIPS, rows // CHIPS, d)
     wide = d // 4
-    whole, small, large = (1, CHIPS, 8, wide), (2, CHIPS, 8, 2 * wide // PARTS), (PARTS, CHIPS, 8, 2 * wide // PARTS)
+    whole, large = (1, CHIPS, 8, wide), (PARTS, CHIPS, 8, 2 * wide // PARTS)
     dma = pltpu.SemaphoreType.DMA
     anywhere = pl.BlockSpec(memory_space=pl.ANY)
     vmem = pl.BlockSpec(memory_space=pltpu.VMEM)
@@ -382,8 +371,8 @@
         pltpu.VMEM((d,), BF16),
         pltpu.VMEM((d,), BF16),
     ]
-    scratch += [pltpu.VMEM(whole, BF16)] * 3 + [pltpu.VMEM(small, BF16)] * 3 + [pltpu.VMEM(large, BF16)] * 3
-    scratch += [dma((3, 8, 2)), dma((4,))] + [dma((1, 8, CHIPS))] + [dma((2, 8, CHIPS)), dma((PARTS, 8, CHIPS))]
+    scratch += [pltpu.VMEM(whole, BF16)] * 6 + [pltpu.VMEM(large, BF16)] * 3
+    scratch += [dma((3, 8, 2)), dma((4,))] + [dma((1, 8, CHIPS))] * 2 + [dma((PARTS, 8, CHIPS))]
     out = pl.pallas_call(
         layer_kernel,
         out_shape=jax.ShapeDtypeStruct(blocks, BF16),

time: 96.7 us -> 95.7 us (0.990)
  Pallas kernels: 94.6 us -> 93.6 us
    pallas_call x1, Pallas kernels: 94.6 us -> 93.6 us  [layer(): pl.pallas_call(layer_kernel, out_shape=jax.ShapeDtypeStruct(blocks, BF16)...]
where the time goes in v5:
time: 95.7 us; the launch traced here: 95.5 us
  Pallas kernels  93.6 us (98%)
  local copies, waits for them, and re-layouts  1.92 us (2%)
    pallas_call x1, Pallas kernels, layer(): pl.pallas_call(layer_kernel, out_shape=jax.ShapeDtypeStruct(blocks, BF16)...  93.6 us
    unnamed x1, local copies, waits for them, and re-layouts  1.92 us

profile of v5, /device:TPU:0, one launch (start us, length us, event | category | flops | bytes accessed | tf_op | source)
XLA Modules:
  0.0 95.5 jit_solution(16939408250612210536)
XLA Ops:
  0.0 93.6 %layer.1 = bf16[8,8,4608]{2,1,0:T(8,128)(2,1)} custom-call(f32[2,128]{1,0:T(2,128)} %constant.2.clone.turn_ref, bf16[8,8,4608]{2,1,0:T(8,128)(2,1)} %bitcast.5, bf16[64,4096,128]{2,1,0:T(8,128)(2,1)} %bitcast.1.k_hbm, bf16[64,4096,128]{2,1,0:T(8,128)(2,1)} %bitcast.2.v_hbm, bf16[4608]{0:T(1024)(128)(2,1)} %ga_hbm.1, bf16[4608,256]{1,0:T(8,128)(2,1)} %wq_hbm.1, ...), custom_call_target="tpu_custom_call" | custom-call | tf_op jit(solution)/shard_map/layer/pallas_call | solution.py:376
  93.6 1.9 %copy.13 = bf16[64,4608]{1,0:T(8,128)(2,1)} copy(bf16[64,4608]{1,0:T(8,128)(2,1)} %bitcast.4) | data formatting | bytes 1179648
